TPU v7x, 32 devices: a 4x2x2 block of a 4x4x8 slice. The times are simulated.
32 devices in a mesh: dp: 4 (over y, z), tp: 8 (over x, core).
Axes of the slice: x: 4, y: 2, z: 2, core: 2. Of those that a mesh axis runs over, the one named last changes fastest.
The devices are a block of a 4x4x8 slice.
Arguments:
- hidden: bfloat16 [16384, 1536], P(('dp', 'tp')), parts along dimension 0
- routes: int32 [2, 16384], P(None, ('dp', 'tp')), parts along dimension 1
- w_query: bfloat16 [2, 1536, 1536], P(None, None, 'tp')
- w_key: bfloat16 [1536, 512], P(None, 'tp')
- w_value: bfloat16 [1536, 512], P(None, 'tp')
- w_out: bfloat16 [2, 1536, 1536], P(None, 'tp')
- q_gain: float32 [2, 64], replicated
- k_gain: float32 [64], replicated
- w_router: bfloat16 [2, 1536, 40], replicated
- shared_gate: bfloat16 [2, 1536, 512], P(None, None, 'tp')
- shared_up: bfloat16 [2, 1536, 512], P(None, None, 'tp')
- shared_down: bfloat16 [2, 512, 1536], P(None, 'tp')
- expert_gate: bfloat16 [2, 40, 1536, 512], P(None, None, None, 'tp')
- expert_up: bfloat16 [2, 40, 1536, 512], P(None, None, None, 'tp')
- expert_down: bfloat16 [2, 40, 512, 1536], P(None, None, 'tp')
Outputs:
- output 1: bfloat16 [16384, 1536], P(('dp', 'tp')), parts along dimension 0
- output 2: bfloat16 [16384, 8, 64], P('dp', 'tp'), parts along dimension 0
- output 3: bfloat16 [16384, 8, 64], P('dp', 'tp'), parts along dimension 0
There are 4 independent parts. A program takes and returns all parts, laid end to end along the dimension named above; an argument that names none is the same for every part.
All inputs are finite; a program needn't handle non-finite values.
Results may differ from a plain program's by a relative error of at most 0.02.
Values are sent between devices in bfloat16 or wider.
A program may use at most 768 MiB of HBM per device.

v0:
```python
import jax
import jax.numpy as jnp
from jax import lax
from jax.sharding import PartitionSpec as P

EPS = 1e-5
ROPE_BASE = 10000.0
Q_BLOCK = 256


def rms_norm(vals):
    vals = vals.astype(jnp.float32)
    return vals * lax.rsqrt(jnp.mean(vals * vals, axis=-1, keepdims=True) + EPS)


def rope_tables(seq_len, head_dim):
    half_dim = head_dim // 2
    inv_freq = ROPE_BASE ** (-2.0 * jnp.arange(half_dim, dtype=jnp.float32) / head_dim)
    angles = jnp.arange(seq_len, dtype=jnp.float32)[:, None] * inv_freq[None, :]
    return jnp.cos(angles)[:, None, :], jnp.sin(angles)[:, None, :]


def rope_norm(vals, cos_t, sin_t, gain):
    vals = vals.astype(jnp.float32)
    half_dim = vals.shape[-1] // 2
    first, second = vals[..., :half_dim], vals[..., half_dim:]
    rotated = jnp.concatenate([first * cos_t - second * sin_t, second * cos_t + first * sin_t], axis=-1)
    return (rms_norm(rotated) * gain).astype(jnp.bfloat16)


def causal_attention(q_n, k_n, v_heads):
    seq_len, heads_loc, head_dim = q_n.shape
    kv_loc = k_n.shape[1]
    n_blocks = seq_len // Q_BLOCK
    q_blocks = q_n.reshape(n_blocks, Q_BLOCK, kv_loc, heads_loc // kv_loc, head_dim)
    key_pos = jnp.arange(seq_len)

    def one_block(operands):
        q_blk, blk_start = operands
        scores = jnp.einsum("qkgd,skd->kgqs", q_blk, k_n, preferred_element_type=jnp.float32) * head_dim ** -0.5
        causal_mask = key_pos[None, :] <= (blk_start + jnp.arange(Q_BLOCK))[:, None]
        attn_probs = jax.nn.softmax(jnp.where(causal_mask, scores, -jnp.inf), axis=-1).astype(jnp.bfloat16)
        blk_out = jnp.einsum("kgqs,skd->qkgd", attn_probs, v_heads, preferred_element_type=jnp.float32)
        return blk_out.astype(jnp.bfloat16).reshape(Q_BLOCK, heads_loc * head_dim)

    blk_outs = lax.map(one_block, (q_blocks, jnp.arange(n_blocks) * Q_BLOCK))
    return blk_outs.reshape(seq_len, heads_loc * head_dim)


def routed_experts(n_rows, route, gate_val, e_gate, e_up, e_down):
    n_experts = e_gate.shape[0]
    counts = jnp.bincount(route, length=n_experts).astype(jnp.int32)
    order = jnp.argsort(route, stable=True)
    inverse = jnp.zeros_like(order).at[order].set(jnp.arange(order.shape[0], dtype=order.dtype))
    sorted_rows = jnp.take(n_rows, order, axis=0)
    gate_part = lax.ragged_dot(sorted_rows, e_gate, counts, preferred_element_type=jnp.float32)
    up_part = lax.ragged_dot(sorted_rows, e_up, counts, preferred_element_type=jnp.float32)
    mid_act = (jax.nn.silu(gate_part) * up_part).astype(jnp.bfloat16)
    sorted_out = lax.ragged_dot(mid_act, e_down, counts, preferred_element_type=jnp.float32)
    return jnp.take(sorted_out, inverse, axis=0) * gate_val[:, None]


def moe_partial(n_rows, route, router_w, s_gate, s_up, s_down, e_gate, e_up, e_down):
    n_experts = router_w.shape[1]
    router_probs = jax.nn.softmax(jnp.dot(n_rows, router_w, preferred_element_type=jnp.float32), axis=-1)
    gate_val = jnp.sum(jnp.where(route[:, None] == jnp.arange(n_experts)[None, :], router_probs, 0.0), axis=1)
    shared_mid = (jax.nn.silu(jnp.dot(n_rows, s_gate, preferred_element_type=jnp.float32)) * jnp.dot(n_rows, s_up, preferred_element_type=jnp.float32)).astype(jnp.bfloat16)
    shared_out = jnp.dot(shared_mid, s_down, preferred_element_type=jnp.float32)
    return shared_out + routed_experts(n_rows, route, gate_val, e_gate, e_up, e_down)


def solution(mesh):
    seq_spec = P(("dp", "tp"), None)
    in_specs = (seq_spec, P(None, ("dp", "tp")), P(None, None, "tp"), P(None, "tp"), P(None, "tp"), P(None, "tp", None), P(None, None), P(None), P(None, None, None), P(None, None, "tp"), P(None, None, "tp"), P(None, "tp", None), P(None, None, None, "tp"), P(None, None, None, "tp"), P(None, None, "tp", None))
    out_specs = (seq_spec, P("dp", "tp", None), P("dp", "tp", None))

    def per_device(hidden, routes, w_query, w_key, w_value, w_out, q_gain, k_gain, w_router, shared_gate, shared_up, shared_down, expert_gate, expert_up, expert_down):
        head_dim = q_gain.shape[1]
        routes_all = lax.all_gather(routes, "tp", axis=1, tiled=True)
        seq_len = routes_all.shape[1]
        cos_t, sin_t = rope_tables(seq_len, head_dim)
        state = hidden
        for layer in range(2):
            a_all = lax.all_gather(rms_norm(state).astype(jnp.bfloat16), "tp", axis=0, tiled=True)
            if layer == 0:
                k_proj = jnp.dot(a_all, w_key, preferred_element_type=jnp.float32).astype(jnp.bfloat16)
                k_cache = rope_norm(k_proj.reshape(seq_len, -1, head_dim), cos_t, sin_t, k_gain)
                v_cache = jnp.dot(a_all, w_value, preferred_element_type=jnp.float32).astype(jnp.bfloat16).reshape(seq_len, -1, head_dim)
            q_heads = jnp.dot(a_all, w_query[layer], preferred_element_type=jnp.float32).astype(jnp.bfloat16).reshape(seq_len, -1, head_dim)
            attn_out = causal_attention(rope_norm(q_heads, cos_t, sin_t, q_gain[layer]), k_cache, v_cache)
            attn_part = jnp.dot(attn_out, w_out[layer], preferred_element_type=jnp.float32).astype(jnp.bfloat16)
            attn_sum = lax.psum_scatter(attn_part, "tp", scatter_dimension=0, tiled=True)
            state = (state.astype(jnp.float32) + attn_sum.astype(jnp.float32)).astype(jnp.bfloat16)
            n_all = lax.all_gather(rms_norm(state).astype(jnp.bfloat16), "tp", axis=0, tiled=True)
            moe_part = moe_partial(n_all, routes_all[layer], w_router[layer], shared_gate[layer], shared_up[layer], shared_down[layer], expert_gate[layer], expert_up[layer], expert_down[layer]).astype(jnp.bfloat16)
            moe_sum = lax.psum_scatter(moe_part, "tp", scatter_dimension=0, tiled=True)
            state = (state.astype(jnp.float32) + moe_sum.astype(jnp.float32)).astype(jnp.bfloat16)
        return (state, k_cache, v_cache)

    return jax.shard_map(per_device, mesh=mesh, in_specs=in_specs, out_specs=out_specs, check_vma=False)
```

profile of v0, /device:TPU:81, one launch (start us, length us, event | category | flops | bytes accessed | tf_op | source)
XLA Modules:
  0.0 1983.1 jit_solution(1482136262327123039)
XLA Ops:
  14.7 66.3 %all-gather.5.cloned.1.call-done = bf16[4096,1536]{1,0:T(8,128)(2,1)} async-done(((bf16[512,1536]{1,0:T(8,128)(2,1)}), bf16[4096,1536]{1,0:T(8,128)(2,1)}) %all-gather.5.cloned.1.call-update) | async-done | bytes 12582928 | tf_op jit(solution)/shard_map/all_gather | solution.py:84
  81.1 8.8 convolution_convert_fusion.3
  107.7 383.1 %while.22 = (s32[]{:T(128)}, bf16[16,256,192]{1,2,0:T(8,128)(2,1)S(1)}, s32[16]{0:T(128)S(1)}, bf16[16,256,1,3,64]{1,4,3,2,0:T(8,128)(2,1)S(1)}, bf16[4096,1,64]...) while((s32[]{:T(128)}, bf16[16,256,192]{1,2,0:T(8,128)(2,1)S(1)}, s32[16]{0:T(128)S(1)}, ...), condition=%wide.region_6.7_spmd.clone, body=%wide.region_3.6_spmd.clone.sunk | while | flops 844151552 | bytes 45499520 | solution.py:46
  116.6 8.3 fusion.156
  140.6 8.3 fusion.156
  164.5 8.3 fusion.156
  188.5 8.3 fusion.156
  212.4 8.3 fusion.156
  236.3 8.3 fusion.156
  260.3 8.3 fusion.156
  284.2 8.3 fusion.156
  308.2 8.3 fusion.156
  332.1 8.3 fusion.156
  498.9 69.0 %reduce-scatter.5.cloned.1.call-done = bf16[512,1536]{1,0:T(8,128)(2,1)} async-done(((bf16[4096,1536]{1,0:T(8,128)(2,1)}), bf16[512,1536]{1,0:T(8,128)(2,1)}) %reduce-scatter.5.cloned.1.call-update) | async-done | bytes 1572880 | tf_op jit(solution)/shard_map/reduce_scatter | solution.py:92
  571.7 13.9 all_gather.17
  586.3 29.3 %scatter_custom_fusion = s32[40]{0:T(128)} fusion(s32[4096]{0:T(1024)S(1)} %bitcast.284, s32[4096]{0:T(1024)S(1)} %broadcast.306, s32[]{:T(128)} %constant.54.clone.1), kind=kCustom, calls=%fused_computation.203 | custom fusion | flops 4096 | bytes 164 | tf_op jit(solution)/shard_map/scatter-add | solution.py:52
  618.4 11.0 fusion.124
  629.4 15.0 copy.40
  644.4 11.1 fusion.125
  655.5 15.0 copy.41
  676.3 15.5 scatter_custom_fusion.1
  691.9 11.3 slice_bitcast_fusion
  703.2 31.5 %gather_fusion = bf16[4096,1536]{1,0:T(8,128)(2,1)} fusion(bf16[4096,1536]{1,0:T(8,128)(2,1)} %all-gather.7.cloned.1.call-done, s32[4096]{0:T(1024)S(1)} %get-tuple-element.198), kind=kCustom, calls=%fused_computation.clone | custom fusion | bytes 25182208 | tf_op jit(solution)/shard_map/jit(_take)/gather | solution.py:55
  734.7 11.2 broadcast_select_fusion.1
  745.8 43.6 %ragged-dot-none.5 = f32[4096,64]{1,0:T(8,128)} custom-call(s32[1]{0:T(128)} %get-tuple-element.97, s32[41]{0:T(128)} %get-tuple-element.98, s32[55]{0:T(128)} %get-tuple-element.99, s32[55]{0:T(128)} %get-tuple-element.100, s32[1]{0:T(128)} %get-tuple-element.97, bf16[4096,1536]{1,0:T(8,128)(2,1)} %broadcast_select_fusion.1, bf16[40,1536,64]{2,1,0:T(8,128)(2,1)} %bitcast.257), custom_call_target="tpu_custom_call" | custom-call | flops 805306368 | bytes 21495968 | tf_op jit(solution)/shard_map/ragged_dot_general/ragged-dot-none
  789.5 43.7 %ragged-dot-none.4 = f32[4096,64]{1,0:T(8,128)} custom-call(s32[1]{0:T(128)} %get-tuple-element.97, s32[41]{0:T(128)} %get-tuple-element.98, s32[55]{0:T(128)} %get-tuple-element.99, s32[55]{0:T(128)} %get-tuple-element.100, s32[1]{0:T(128)} %get-tuple-element.97, bf16[4096,1536]{1,0:T(8,128)(2,1)} %broadcast_select_fusion.1, bf16[40,1536,64]{2,1,0:T(8,128)(2,1)} %bitcast.258), custom_call_target="tpu_custom_call" | custom-call | flops 805306368 | bytes 21495968 | tf_op jit(solution)/shard_map/ragged_dot_general/ragged-dot-none
  833.2 8.5 fusion.127
  843.5 44.2 %ragged-dot-none.3 = f32[4096,1536]{1,0:T(8,128)} custom-call(s32[1]{0:T(128)} %get-tuple-element.97, s32[41]{0:T(128)} %get-tuple-element.98, s32[55]{0:T(128)} %get-tuple-element.99, s32[55]{0:T(128)} %get-tuple-element.100, s32[1]{0:T(128)} %get-tuple-element.97, bf16[4096,64]{1,0:T(8,128)(2,1)} %multiply_convert_fusion.1, ...), custom_call_target="tpu_custom_call" | custom-call | flops 805306368 | bytes 33554592 | tf_op jit(solution)/shard_map/ragged_dot_general/ragged-dot-none
  887.7 35.8 %gather_fusion.1 = f32[4096,1536]{1,0:T(8,128)} fusion(f32[4096,1536]{1,0:T(8,128)} %ragged-dot-none.3, s32[4096]{0:T(1024)S(1)} %fusion.111), kind=kCustom, calls=%fused_computation.1.clone | custom fusion | bytes 50348032 | tf_op jit(solution)/shard_map/jit(_take)/gather | solution.py:60
  930.1 23.2 %fusion.37 = bf16[4096,1536]{1,0:T(8,128)(2,1)} fusion(f32[4096,1536]{1,0:T(8,128)} %gather_fusion.1, f32[4096]{0:T(1024)S(1)} %select_reduce_fusion.1, pred[4096]{0:T(1024)(128)(4,1)S(1)} %compare_and_fusion.2, bf16[4096,1536]{1,0:T(8,128)(2,1)} %all-gather.7.cloned.1.call-done, f32[4096,64]{1,0:T(8,128)S(1)} %fusion.95, ...), kind=kOutput, calls=%fused_computation.53 | convolution fusion | flops 1637351424 | bytes 52842496 | tf_op jit(solution)/shard_map/dot_general | solution.py:68
  953.4 67.3 %reduce-scatter.7.cloned.1.call-done = bf16[512,1536]{1,0:T(8,128)(2,1)} async-done(((bf16[4096,1536]{1,0:T(8,128)(2,1)}), bf16[512,1536]{1,0:T(8,128)(2,1)}) %reduce-scatter.7.cloned.1.call-update) | async-done | bytes 1572880 | tf_op jit(solution)/shard_map/reduce_scatter | solution.py:96
  1025.8 64.8 %all-gather.9.cloned.1.call-done = bf16[4096,1536]{1,0:T(8,128)(2,1)} async-done(((bf16[512,1536]{1,0:T(8,128)(2,1)}), bf16[4096,1536]{1,0:T(8,128)(2,1)}) %all-gather.9.cloned.1.call-update) | async-done | bytes 12582928 | tf_op jit(solution)/shard_map/all_gather | solution.py:84
  1090.6 8.8 convolution_convert_fusion.2
  1103.6 383.2 %while.23 = (s32[]{:T(128)}, bf16[16,256,192]{1,2,0:T(8,128)(2,1)S(1)}, s32[16]{0:T(128)S(1)}, bf16[16,256,1,3,64]{1,4,3,2,0:T(8,128)(2,1)S(1)}, bf16[4096,1,64]...) while((s32[]{:T(128)}, bf16[16,256,192]{1,2,0:T(8,128)(2,1)S(1)}, ...), condition=%wide.region_21.24_spmd.clone, body=%wide.region_18.23_spmd.clone.sunk | while | flops 844151552 | bytes 45499520 | solution.py:46
  1494.7 69.0 %reduce-scatter.9.cloned.1.call-done = bf16[512,1536]{1,0:T(8,128)(2,1)} async-done(((bf16[4096,1536]{1,0:T(8,128)(2,1)}), bf16[512,1536]{1,0:T(8,128)(2,1)}) %reduce-scatter.9.cloned.1.call-update) | async-done | bytes 1572880 | tf_op jit(solution)/shard_map/reduce_scatter | solution.py:92
  1567.6 29.5 %scatter_custom_fusion.2 = s32[40]{0:T(128)} fusion(s32[4096]{0:T(1024)} %bitcast.283, s32[4096]{0:T(1024)} %copy-done.32, s32[]{:T(128)} %constant.54.clone.1), kind=kCustom, calls=%fused_computation.201 | custom fusion | flops 4096 | bytes 672 | tf_op jit(solution)/shard_map/scatter-add | solution.py:52
  1600.0 15.0 copy.42
  1615.0 15.1 copy.43
  1635.9 15.5 scatter_custom_fusion.3
  1651.5 8.3 fusion.128
  1660.2 31.5 %gather_fusion.2 = bf16[4096,1536]{1,0:T(8,128)(2,1)} fusion(bf16[4096,1536]{1,0:T(8,128)(2,1)} %all-gather.11.cloned.1.call-done, s32[4096]{0:T(1024)S(1)} %get-tuple-element.196), kind=kCustom, calls=%fused_computation.2.clone | custom fusion | bytes 25182208 | tf_op jit(solution)/shard_map/jit(_take)/gather | solution.py:55
  1691.7 11.2 broadcast_select_fusion
  1702.9 43.6 %ragged-dot-none.2 = f32[4096,64]{1,0:T(8,128)} custom-call(s32[1]{0:T(128)} %get-tuple-element.85, s32[41]{0:T(128)} %get-tuple-element.86, s32[55]{0:T(128)} %get-tuple-element.87, s32[55]{0:T(128)} %get-tuple-element.88, s32[1]{0:T(128)} %get-tuple-element.85, bf16[4096,1536]{1,0:T(8,128)(2,1)} %broadcast_select_fusion, bf16[40,1536,64]{2,1,0:T(8,128)(2,1)} %bitcast.255), custom_call_target="tpu_custom_call" | custom-call | flops 805306368 | bytes 21495968 | tf_op jit(solution)/shard_map/ragged_dot_general/ragged-dot-none
  1746.5 43.7 %ragged-dot-none.1 = f32[4096,64]{1,0:T(8,128)} custom-call(s32[1]{0:T(128)} %get-tuple-element.85, s32[41]{0:T(128)} %get-tuple-element.86, s32[55]{0:T(128)} %get-tuple-element.87, s32[55]{0:T(128)} %get-tuple-element.88, s32[1]{0:T(128)} %get-tuple-element.85, bf16[4096,1536]{1,0:T(8,128)(2,1)} %broadcast_select_fusion, bf16[40,1536,64]{2,1,0:T(8,128)(2,1)} %bitcast.256), custom_call_target="tpu_custom_call" | custom-call | flops 805306368 | bytes 21495968 | tf_op jit(solution)/shard_map/ragged_dot_general/ragged-dot-none
  1793.3 44.2 %ragged-dot-none = f32[4096,1536]{1,0:T(8,128)} custom-call(s32[1]{0:T(128)} %get-tuple-element.85, s32[41]{0:T(128)} %get-tuple-element.86, s32[55]{0:T(128)} %get-tuple-element.87, s32[55]{0:T(128)} %get-tuple-element.88, s32[1]{0:T(128)} %get-tuple-element.85, bf16[4096,64]{1,0:T(8,128)(2,1)} %multiply_convert_fusion, ...), custom_call_target="tpu_custom_call" | custom-call | flops 805306368 | bytes 33554592 | tf_op jit(solution)/shard_map/ragged_dot_general/ragged-dot-none
  1837.5 35.6 %gather_fusion.3 = f32[4096,1536]{1,0:T(8,128)} fusion(f32[4096,1536]{1,0:T(8,128)} %ragged-dot-none, s32[4096]{0:T(1024)S(1)} %fusion.112), kind=kCustom, calls=%fused_computation.3.clone | custom fusion | bytes 50348032 | tf_op jit(solution)/shard_map/jit(_take)/gather | solution.py:60
  1879.7 23.2 %fusion.35 = bf16[4096,1536]{1,0:T(8,128)(2,1)} fusion(f32[4096,1536]{1,0:T(8,128)} %gather_fusion.3, f32[4096]{0:T(1024)S(1)} %select_reduce_fusion, pred[4096]{0:T(1024)(128)(4,1)S(1)} %compare_and_fusion, bf16[4096,1536]{1,0:T(8,128)(2,1)} %all-gather.11.cloned.1.call-done, f32[4096,64]{1,0:T(8,128)S(1)} %fusion.90, ...), kind=kOutput, calls=%fused_computation.50 | convolution fusion | flops 1637351424 | bytes 52842496 | tf_op jit(solution)/shard_map/dot_general | solution.py:68
  1903.0 69.7 %reduce-scatter.11.cloned.1.call-done = bf16[512,1536]{1,0:T(8,128)(2,1)} async-done(((bf16[4096,1536]{1,0:T(8,128)(2,1)}), bf16[512,1536]{1,0:T(8,128)(2,1)}) %reduce-scatter.11.cloned.1.call-update) | async-done | bytes 1572880 | tf_op jit(solution)/shard_map/reduce_scatter | solution.py:96
  (454 shorter events, 779.2 us)
Async XLA Ops:
  7.2 85.9 %copy-start = (bf16[1536,64]{0,1:T(8,128)(2,1)S(1)}, bf16[1536,64]{0,1:T(8,128)(2,1)}, u32[]{:S(2)}) copy-start(bf16[1536,64]{0,1:T(8,128)(2,1)} %param.26) | copy-start | bytes 589828
  7.2 73.9 %all-gather.5.cloned.1.call-start = ((), (), s32[]{:S(2)}) async-start(), calls=%async_computation.4 | async-start | bytes 14155776 | tf_op jit(solution)/shard_map/all_gather | solution.py:84
  9.1 72.0 %copy-start.37 = (bf16[2,1536,192]{1,2,0:T(8,128)(2,1)S(1)}, bf16[2,1536,192]{1,2,0:T(8,128)(2,1)}, u32[]{:S(2)}) copy-start(bf16[2,1536,192]{1,2,0:T(8,128)(2,1)} %param.25) | copy-start | bytes 3538948
  12.1 555.7 %reduce-scatter.5.cloned.1.call-start = ((), (), s32[]{:S(2)}) async-start(), calls=%async_computation.5 | async-start | bytes 14155776 | tf_op jit(solution)/shard_map/reduce_scatter | solution.py:92
  14.7 75.5 %copy-start.14 = (f32[4096,32]{0,1:T(8,128)}, f32[4096,32]{0,1:T(8,128)S(1)}, u32[]{:S(2)}) copy-start(f32[4096,32]{0,1:T(8,128)S(1)} %get-tuple-element.201) | copy-start | bytes 1572868
  14.7 75.5 %copy-start.16 = (f32[4096,32]{0,1:T(8,128)}, f32[4096,32]{0,1:T(8,128)S(1)}, u32[]{:S(2)}) copy-start(f32[4096,32]{0,1:T(8,128)S(1)} %get-tuple-element.202) | copy-start | bytes 1572868
  140.6 8.3 copy-start.22
  164.5 8.3 copy-start.22
  188.5 8.3 copy-start.22
  212.4 8.3 copy-start.22
  236.3 8.3 copy-start.22
  260.3 8.3 copy-start.22
  284.2 8.3 copy-start.22
  332.1 8.3 copy-start.22
  356.0 8.3 copy-start.22
  380.0 8.3 copy-start.22
  403.9 8.3 copy-start.22
  427.9 8.3 copy-start.22
  451.8 8.3 copy-start.22
  475.7 8.3 copy-start.22
  498.7 69.1 %copy-start.2 = (bf16[512,1536]{1,0:T(8,128)(2,1)S(1)}, bf16[512,1536]{1,0:T(8,128)(2,1)}, u32[]{:S(2)}) copy-start(bf16[512,1536]{1,0:T(8,128)(2,1)} %param.23) | copy-start | bytes 4718596
  498.8 204.4 %all-gather.7.cloned.1.call-start = ((), (), s32[]{:S(2)}) async-start(), calls=%async_computation.6 | async-start | bytes 14155776 | tf_op jit(solution)/shard_map/all_gather | solution.py:94
  571.7 449.0 %reduce-scatter.7.cloned.1.call-start = ((), (), s32[]{:S(2)}) async-start(), calls=%async_computation.7 | async-start | bytes 14155776 | tf_op jit(solution)/shard_map/reduce_scatter | solution.py:96
  586.3 43.1 %copy-start.32 = (s32[4096]{0:T(1024)}, s32[4096]{0:T(1024)S(1)}, u32[]{:S(2)}) copy-start(s32[4096]{0:T(1024)S(1)} %broadcast.306) | copy-start | bytes 49156
  789.5 43.7 %copy-start.28 = (bf16[2,1536,40]{1,2,0:T(8,128)(2,1)S(1)}, bf16[2,1536,40]{1,2,0:T(8,128)(2,1)}, u32[]{:S(2)}) copy-start(bf16[2,1536,40]{1,2,0:T(8,128)(2,1)} %param.31) | copy-start | bytes 737284
  833.2 8.8 copy-start.11
  833.2 8.8 copy-start.12
  887.7 35.8 %copy-start.24 = (bf16[2,1536,64]{1,2,0:T(8,128)(2,1)S(1)}, bf16[2,1536,64]{1,2,0:T(8,128)(2,1)}, u32[]{:S(2)}) copy-start(bf16[2,1536,64]{1,2,0:T(8,128)(2,1)} %param.32) | copy-start | bytes 1179652
  953.3 67.4 %copy-start.3 = (bf16[512,1536]{1,0:T(8,128)(2,1)S(1)}, bf16[512,1536]{1,0:T(8,128)(2,1)}, u32[]{:S(2)}) copy-start(bf16[512,1536]{1,0:T(8,128)(2,1)} %param.23) | copy-start | bytes 4718596
  953.3 67.4 %copy-start.8 = (bf16[512,1536]{1,0:T(8,128)(2,1)S(1)}, bf16[512,1536]{1,0:T(8,128)(2,1)}, u32[]{:S(2)}) copy-start(bf16[512,1536]{1,0:T(8,128)(2,1)} %reduce-scatter.5.cloned.1.call-done) | copy-start | bytes 4718596
  953.3 137.3 %all-gather.9.cloned.1.call-start = ((), (), s32[]{:S(2)}) async-start(), calls=%async_computation.8 | async-start | bytes 14155776 | tf_op jit(solution)/shard_map/all_gather | solution.py:84
  1023.0 67.6 %copy-start.38 = (bf16[2,1536,192]{1,2,0:T(8,128)(2,1)S(1)}, bf16[2,1536,192]{1,2,0:T(8,128)(2,1)}, u32[]{:S(2)}) copy-start(bf16[2,1536,192]{1,2,0:T(8,128)(2,1)} %param.25) | copy-start | bytes 3538948
  1025.7 537.9 %reduce-scatter.9.cloned.1.call-start = ((), (), s32[]{:S(2)}) async-start(), calls=%async_computation.9 | async-start | bytes 14155776 | tf_op jit(solution)/shard_map/reduce_scatter | solution.py:92
  1112.7 8.3 copy-start.23
  1136.6 8.3 copy-start.23
  1160.5 8.3 copy-start.23
  1208.4 8.3 copy-start.23
  1232.4 8.3 copy-start.23
  1494.6 69.1 %copy-start.5 = (bf16[512,1536]{1,0:T(8,128)(2,1)S(1)}, bf16[512,1536]{1,0:T(8,128)(2,1)}, u32[]{:S(2)}) copy-start(bf16[512,1536]{1,0:T(8,128)(2,1)} %copy-done.4) | copy-start | bytes 4718596
  1494.6 156.9 %all-gather.11.cloned.1.call-start = ((), (), s32[]{:S(2)}) async-start(), calls=%async_computation.10 | async-start | bytes 14155776 | tf_op jit(solution)/shard_map/all_gather | solution.py:94
  1567.5 405.2 %reduce-scatter.11.cloned.1.call-start = ((), (), s32[]{:S(2)}) async-start(), calls=%async_computation.11 | async-start | bytes 14155776 | tf_op jit(solution)/shard_map/reduce_scatter | solution.py:96
  1615.0 15.1 copy-start.31
  1615.0 36.5 %copy-start.29 = (bf16[2,1536,40]{1,2,0:T(8,128)(2,1)S(1)}, bf16[2,1536,40]{1,2,0:T(8,128)(2,1)}, u32[]{:S(2)}) copy-start(bf16[2,1536,40]{1,2,0:T(8,128)(2,1)} %param.31) | copy-start | bytes 737284
  1746.5 43.7 %copy-start.13 = (f32[4096,64]{1,0:T(8,128)S(1)}, f32[4096,64]{1,0:T(8,128)}, u32[]{:S(2)}) copy-start(f32[4096,64]{1,0:T(8,128)} %ragged-dot-none.2) | copy-start | bytes 3145732
  1837.5 35.7 %copy-start.25 = (bf16[2,1536,64]{1,2,0:T(8,128)(2,1)S(1)}, bf16[2,1536,64]{1,2,0:T(8,128)(2,1)}, u32[]{:S(2)}) copy-start(bf16[2,1536,64]{1,2,0:T(8,128)(2,1)} %param.32) | copy-start | bytes 1179652
  1902.9 69.7 %copy-start.6 = (bf16[512,1536]{1,0:T(8,128)(2,1)S(1)}, bf16[512,1536]{1,0:T(8,128)(2,1)}, u32[]{:S(2)}) copy-start(bf16[512,1536]{1,0:T(8,128)(2,1)} %copy-done.4) | copy-start | bytes 4718596
  1902.9 69.7 %copy-start.10 = (bf16[512,1536]{1,0:T(8,128)(2,1)S(1)}, bf16[512,1536]{1,0:T(8,128)(2,1)}, u32[]{:S(2)}) copy-start(bf16[512,1536]{1,0:T(8,128)(2,1)} %reduce-scatter.9.cloned.1.call-done) | copy-start | bytes 4718596
  1903.0 72.8 %copy-start.1 = (bf16[1536,64]{0,1:T(8,128)(2,1)S(1)}, bf16[1536,64]{0,1:T(8,128)(2,1)}, u32[]{:S(2)}) copy-start(bf16[1536,64]{0,1:T(8,128)(2,1)} %param.26) | copy-start | bytes 589828
  (34 other events, 176.7 us)
Sparse Core Ops, SparseCore 0:
  12.2 68.7 all-gather.4
  498.9 68.8 reduce-scatter.4
  571.8 64.7 all-gather.6
  953.5 67.1 reduce-scatter.6
  1025.8 64.7 all-gather.8
  1494.7 68.8 reduce-scatter.8
  1567.6 65.1 all-gather.10
  1903.1 69.5 reduce-scatter.10
where the time goes:
time: 2000 us; the launch traced here: 1980 us
  matrix products  553 us (28%)
  other arithmetic  434 us (22%)
  waiting for transfers between devices  406 us (20%)
  local copies, waits for them, and re-layouts  289 us (14%)
  Pallas kernels  269 us (13%)
    reduce_sum x32, other arithmetic, one_block(): jax.nn.softmax(jnp.where(causal_mask, scores, -jnp.inf), axis=-1)  265 us
    another operation x6, Pallas kernels  263 us
    dot_general x32, matrix products, one_block(): jnp.einsum('qkgd,skd->kgqs', q_blk, k_n, preferred_element_type=jnp.float32)  224 us
    dot_general x32, matrix products, one_block(): jnp.einsum('kgqs,skd->qkgd', attn_probs, v_heads, preferred_element_type=...  214 us
    reduce_scatter x2, waiting for transfers between devices, per_device(): lax.psum_scatter(attn_part, 'tp', scatter_dimension=0, tiled=True)  138 us
    reduce_scatter x2, waiting for transfers between devices, per_device(): moe_sum = lax.psum_scatter(moe_part, 'tp', scatter_dimension=0, tiled=True)  137 us
    all_gather x4, waiting for transfers between devices, per_device(): lax.all_gather(rms_norm(state).astype(jnp.bfloat16), 'tp', axis=0, tiled=...  131 us
    gather x2, local copies, waits for them, and re-layouts, routed_experts(): return jnp.take(sorted_out, inverse, axis=0) * gate_val[:, None]  71.4 us
  transfers between devices with their start and end apart: 8, of which 6 were waited for; matrix products, arithmetic and copies ran while one was open for 10% of the time, Pallas kernels for 0%

commit v1 on v0

v1 whole, which is shorter than its diff:
```python
import functools
import math

import jax
import jax.numpy as jnp
from jax import lax
from jax.experimental import pallas as pl
from jax.experimental.pallas import tpu as pltpu
from jax.sharding import PartitionSpec as P

EPS = 1e-5
ROPE_BASE = 10000.0
TILE = 16
BLOCK_TILES = 16
GROUP = 4
SCORE_BOUND = 40.0
VALUE_BOUND = 1e15
NEG = -3e38
NT = (((1,), (1,)), ((), ()))
TN = (((0,), (0,)), ((), ()))


def rms_norm(vals):
    vals = vals.astype(jnp.float32)
    return vals * lax.rsqrt(jnp.mean(vals * vals, axis=-1, keepdims=True) + EPS)


def rope_tables_t(seq_len, head_dim):
    half_dim = head_dim // 2
    inv_freq = ROPE_BASE ** (-2.0 * jnp.arange(half_dim, dtype=jnp.float32) / head_dim)
    angles = inv_freq[:, None] * jnp.arange(seq_len, dtype=jnp.float32)[None, :]
    return jnp.cos(angles), jnp.sin(angles)


def rope_norm_t(raw, cos_t, sin_t, gain):
    vals = raw.astype(jnp.float32)
    half_dim = vals.shape[0] // 2
    first, second = vals[:half_dim], vals[half_dim:]
    rotated = jnp.concatenate([first * cos_t - second * sin_t, second * cos_t + first * sin_t], axis=0)
    scale = lax.rsqrt(jnp.mean(rotated * rotated, axis=0, keepdims=True) + EPS)
    return rotated * scale * gain


def qkv_kernel(a_ref, wq_ref, wk_ref, wv_ref, cos_ref, sin_ref, kg_ref, q_out, k_out, v_out, w_cat):
    nq, nk = wq_ref.shape[1], wk_ref.shape[0]

    @pl.when(pl.program_id(0) == 0)
    def _():
        w_cat[:nq, :] = wq_ref[0]
        w_cat[nq : nq + nk, :] = wk_ref[...]
        w_cat[nq + nk :, :] = wv_ref[...]

    res = lax.dot_general(w_cat[...], a_ref[...], NT, preferred_element_type=jnp.float32).astype(jnp.bfloat16)
    q_out[0] = res[:nq]
    k_out[...] = rope_norm_t(res[nq : nq + nk], cos_ref[...], sin_ref[...], kg_ref[...]).astype(jnp.bfloat16)
    v_out[...] = res[nq + nk :]


def qkv_proj(a_all, wq_t, wk_t, wv_t, cos_t, sin_t, k_gain, chunks):
    seq, dim = a_all.shape
    rows = seq // chunks
    nq, nk = wq_t.shape[1], wk_t.shape[0]
    half = cos_t.shape[0]
    return pl.pallas_call(
        qkv_kernel,
        grid=(chunks,),
        in_specs=[
            pl.BlockSpec((rows, dim), lambda i: (i, 0)),
            pl.BlockSpec((1, nq, dim), lambda i: (0, 0, 0)),
            pl.BlockSpec((nk, dim), lambda i: (0, 0)),
            pl.BlockSpec((nk, dim), lambda i: (0, 0)),
            pl.BlockSpec((half, rows), lambda i: (0, i)),
            pl.BlockSpec((half, rows), lambda i: (0, i)),
            pl.BlockSpec((nk, 1), lambda i: (0, 0)),
        ],
        out_specs=[
            pl.BlockSpec((1, nq, rows), lambda i: (i, 0, 0)),
            pl.BlockSpec((nk, rows), lambda i: (0, i)),
            pl.BlockSpec((nk, rows), lambda i: (0, i)),
        ],
        out_shape=[
            jax.ShapeDtypeStruct((chunks, nq, rows), jnp.bfloat16),
            jax.ShapeDtypeStruct((nk, seq), jnp.bfloat16),
            jax.ShapeDtypeStruct((nk, seq), jnp.bfloat16),
        ],
        scratch_shapes=[pltpu.VMEM((nq + 2 * nk, dim), jnp.bfloat16)],
        cost_estimate=pl.CostEstimate(flops=2 * seq * dim * (nq + 2 * nk), bytes_accessed=2 * seq * dim, transcendentals=0),
        name="qkv",
    )(a_all, wq_t, wk_t, wv_t, cos_t, sin_t, k_gain[:, None])


def attention_kernel(fast_ref, q_ref, k_ref, v_ref, cos_ref, sin_ref, qg_ref, out_ref, k2, q2, v_aug, acc, m_sc):
    step = pl.program_id(0)
    head_dim = k_ref.shape[0]
    rows = q_ref.shape[2]
    heads = q_ref.shape[1] // head_dim
    tile = rows // 2
    va = v_aug.shape[0]

    @pl.when(step == 0)
    def _():
        v_aug[...] = jnp.zeros_like(v_aug)

    here = pl.multiple_of(step * rows, rows)
    k_t = k_ref[:, pl.ds(here, rows)].astype(jnp.float32)
    k2[pl.ds(here, rows), :] = jnp.concatenate([k_t, k_t], axis=0).T.astype(jnp.bfloat16)
    v_aug[:head_dim, pl.ds(here, rows)] = v_ref[:, pl.ds(here, rows)]
    ones_row = lax.broadcasted_iota(jnp.int32, (va - head_dim, rows), 0) == 0
    v_aug[head_dim:, pl.ds(here, rows)] = jnp.where(ones_row, 1.0, 0.0).astype(jnp.bfloat16)

    for head in range(heads):
        raw = q_ref[0, head * head_dim : (head + 1) * head_dim, :]
        normed = rope_norm_t(raw, cos_ref[...], sin_ref[...], qg_ref[...]).astype(jnp.bfloat16)
        scaled = normed.astype(jnp.float32) * (head_dim**-0.5 * math.log2(math.e))
        high = scaled.astype(jnp.bfloat16)
        low = (scaled - high.astype(jnp.float32)).astype(jnp.bfloat16)
        q2[:head_dim, head * rows : (head + 1) * rows] = high
        q2[head_dim:, head * rows : (head + 1) * rows] = low

    acc[...] = jnp.zeros_like(acc)

    def columns(n):
        return slice(n * tile, (n + 1) * tile)

    def scores(start, n_keys, n):
        return jnp.dot(k2[pl.ds(start, n_keys), :], q2[:, columns(n)], preferred_element_type=jnp.float32)

    def masked(vals, half):
        key_pos = lax.broadcasted_iota(jnp.int32, vals.shape, 0)
        q_pos = lax.broadcasted_iota(jnp.int32, vals.shape, 1) + half * tile
        return jnp.where(key_pos <= q_pos, vals, NEG)

    def values(probs, start, n_keys):
        return jnp.dot(v_aug[:, pl.ds(start, n_keys)], probs.astype(jnp.bfloat16), preferred_element_type=jnp.float32)

    @pl.when(fast_ref[0] == 1)
    def _():
        def block(kb, carry):
            start = pl.multiple_of(kb * rows, rows)
            for n in range(2 * heads):
                acc[:, columns(n)] += values(jnp.exp2(scores(start, rows, n)), start, rows)
            return carry

        lax.fori_loop(0, step, block, 0)
        for n in range(2 * heads):
            n_keys = (n % 2 + 1) * tile
            acc[:, columns(n)] += values(jnp.exp2(masked(scores(here, n_keys, n), n % 2)), here, n_keys)

    @pl.when(fast_ref[0] != 1)
    def _():
        m_sc[...] = jnp.full_like(m_sc, NEG)

        def online(vals, start, n_keys, n):
            old = m_sc[0:1, columns(n)]
            new = jnp.maximum(old, jnp.max(vals, axis=0, keepdims=True))
            m_sc[0:1, columns(n)] = new
            acc[:, columns(n)] = acc[:, columns(n)] * jnp.exp2(old - new) + values(jnp.exp2(vals - new), start, n_keys)

        def block(kb, carry):
            start = pl.multiple_of(kb * rows, rows)
            for n in range(2 * heads):
                online(scores(start, rows, n), start, rows, n)
            return carry

        lax.fori_loop(0, step, block, 0)
        for n in range(2 * heads):
            n_keys = (n % 2 + 1) * tile
            online(masked(scores(here, n_keys, n), n % 2), here, n_keys, n)

    for head in range(heads):
        cols = slice(head * rows, (head + 1) * rows)
        out = acc[:head_dim, cols] / acc[head_dim : head_dim + 1, cols]
        out_ref[0, head * head_dim : (head + 1) * head_dim, :] = out.astype(jnp.bfloat16)


def attention(fast, q_raw, k_t, v_t, cos_t, sin_t, q_gain):
    chunks, nq, rows = q_raw.shape
    head_dim, seq = k_t.shape
    heads = nq // head_dim
    half = cos_t.shape[0]
    va = head_dim + 16
    pairs = heads * seq * seq // 2
    grid_spec = pltpu.PrefetchScalarGridSpec(
        num_scalar_prefetch=1,
        grid=(chunks,),
        in_specs=[
            pl.BlockSpec((1, nq, rows), lambda i, f: (i, 0, 0)),
            pl.BlockSpec((head_dim, seq), lambda i, f: (0, 0)),
            pl.BlockSpec((head_dim, seq), lambda i, f: (0, 0)),
            pl.BlockSpec((half, rows), lambda i, f: (0, i)),
            pl.BlockSpec((half, rows), lambda i, f: (0, i)),
            pl.BlockSpec((head_dim, 1), lambda i, f: (0, 0)),
        ],
        out_specs=pl.BlockSpec((1, nq, rows), lambda i, f: (i, 0, 0)),
        scratch_shapes=[
            pltpu.VMEM((seq, 2 * head_dim), jnp.bfloat16),
            pltpu.VMEM((2 * head_dim, heads * rows), jnp.bfloat16),
            pltpu.VMEM((va, seq), jnp.bfloat16),
            pltpu.VMEM((va, heads * rows), jnp.float32),
            pltpu.VMEM((8, heads * rows), jnp.float32),
        ],
    )
    return pl.pallas_call(
        attention_kernel,
        grid_spec=grid_spec,
        out_shape=jax.ShapeDtypeStruct((chunks, nq, rows), jnp.bfloat16),
        cost_estimate=pl.CostEstimate(flops=pairs * 256 * 4, bytes_accessed=8 * seq * nq, transcendentals=pairs),
        name="attention",
    )(fast, q_raw, k_t, v_t, cos_t, sin_t, q_gain[:, None])


def tile_lists(routes_all, chunks, n_experts):
    layers, seq = routes_all.shape
    rows = seq // chunks
    routes = routes_all.reshape(layers, chunks, rows)
    counts = jnp.sum((routes[..., None] == jnp.arange(n_experts)).astype(jnp.int32), axis=2)
    ends = jnp.cumsum(counts, axis=-1)
    offs = ends - counts
    first = offs // TILE
    n_tiles = jnp.where(counts > 0, (ends + TILE - 1) // TILE - first, 0)
    src = jnp.broadcast_to(jnp.arange(chunks)[None, :, None], counts.shape)

    def flat(vals):
        return jnp.swapaxes(vals, 1, 2).reshape(layers, 1, n_experts * chunks)

    n_tiles = flat(n_tiles)
    list_end = jnp.cumsum(n_tiles, axis=-1)
    list_off = list_end - n_tiles
    length = seq // TILE + chunks * n_experts + BLOCK_TILES
    pos = jnp.arange(length)[None, :, None]
    hit = (list_off <= pos) & (pos < list_end)

    def pick(vals):
        return jnp.sum(jnp.where(hit, vals, 0), axis=-1)

    entry = pick(pos - list_off + 1)
    valid = entry > 0
    local = pick(flat(first)) + entry - 1
    source = pick(flat(src))
    low = jnp.maximum(pick(flat(offs)) - local * TILE, 0)
    high = jnp.minimum(pick(flat(ends)) - local * TILE, TILE)
    tiles = jnp.where(valid, source * (rows // TILE) + local, 0)
    low = jnp.where(valid, low, 0)
    high = jnp.where(valid, high, 0)
    starts = list_off.reshape(layers, n_experts, chunks)[:, :, 0]
    stops = list_end.reshape(layers, n_experts, chunks)[:, :, -1]
    return tiles, low, high, starts, stops


def expert_kernel(tiles_ref, low_ref, high_ref, start_ref, stop_ref, n_hbm, p_hbm, sg_ref, su_ref, sd_ref, g_ref, u_ref, d_ref, out_hbm, n_all, p_all, out_all, w_in, w_out, lhs, fac, sems, out_sem):
    expert = pl.program_id(0)
    chunks = sems.shape[0] - 1
    rows = n_all.shape[0] // chunks
    width = g_ref.shape[2]
    n_rows = lhs.shape[0]
    dummy = n_all.shape[0]

    def n_copy(s):
        part = pl.ds(s * rows, rows)
        return pltpu.make_async_copy(n_hbm.at[pl.ds(s * (rows + TILE), rows), :], n_all.at[part, :], sems.at[s])

    p_copy = pltpu.make_async_copy(p_hbm, p_all, sems.at[chunks])

    @pl.when(expert == 0)
    def _():
        for s in range(chunks):
            n_copy(s).start()
        p_copy.start()
        w_in[width : 2 * width, :] = sg_ref[0]
        w_in[3 * width :, :] = su_ref[0]
        w_out[width : 2 * width, :] = sd_ref[0]
        w_out[3 * width :, :] = jnp.zeros_like(sd_ref[0])

        def clear(i, carry):
            out_all[pl.ds(pl.multiple_of(i * TILE, TILE), TILE), :] = jnp.zeros((TILE, out_all.shape[1]), out_all.dtype)
            return carry

        lax.fori_loop(0, out_all.shape[0] // TILE, clear, 0)
        for s in range(chunks):
            n_copy(s).wait()
        p_copy.wait()

    w_in[:width, :] = g_ref[0, 0]
    w_in[2 * width : 3 * width, :] = u_ref[0, 0]
    w_out[:width, :] = d_ref[0, 0]
    w_out[2 * width : 3 * width, :] = d_ref[0, 0]

    start, stop = start_ref[expert], stop_ref[expert]
    routed = lax.broadcasted_iota(jnp.int32, (TILE, 2 * width), 1) < width
    row_id = lax.broadcasted_iota(jnp.int32, (TILE, 2 * width), 0)

    def block(b, carry):
        first = start + b * BLOCK_TILES
        for j in range(BLOCK_TILES):
            idx = first + j
            at = pl.ds(pl.multiple_of(tiles_ref[idx] * TILE, TILE), TILE)
            mine = (row_id >= low_ref[idx]) & (row_id < jnp.where(idx < stop, high_ref[idx], 0))
            lhs[j * TILE : (j + 1) * TILE, :] = n_all[at, :]
            fac[j * TILE : (j + 1) * TILE, :] = jnp.where(mine, jnp.where(routed, p_all[at, :], 1.0), 0.0)
        both = lax.dot_general(lhs[...], w_in[...], NT, preferred_element_type=jnp.float32)
        gate, up = both[:, : 2 * width], both[:, 2 * width :]
        mid = (gate * jax.nn.sigmoid(gate) * up).astype(jnp.bfloat16).astype(jnp.float32) * fac[...]
        high = mid.astype(jnp.bfloat16)
        low = (mid - high.astype(jnp.float32)).astype(jnp.bfloat16)
        part = jnp.dot(jnp.concatenate([high, low], axis=1), w_out[...], preferred_element_type=jnp.float32).astype(jnp.bfloat16)
        for j0 in range(0, BLOCK_TILES, GROUP):
            places, sums = [], []
            for j in range(j0, j0 + GROUP):
                idx = first + j
                place = pl.ds(pl.multiple_of(jnp.where(idx < stop, tiles_ref[idx] * TILE, dummy), TILE), TILE)
                places.append(place)
                sums.append(out_all[place, :] + part[j * TILE : (j + 1) * TILE, :])
            for place, total in zip(places, sums):
                out_all[place, :] = total
        return carry

    lax.fori_loop(0, (stop - start + BLOCK_TILES - 1) // BLOCK_TILES, block, 0)

    @pl.when(expert == pl.num_programs(0) - 1)
    def _():
        copy = pltpu.make_async_copy(out_all.at[pl.ds(0, n_all.shape[0]), :], out_hbm, out_sem)
        copy.start()
        copy.wait()


def experts(lists, layer, n_all, p_all, s_gate, s_up, s_down, e_gate, e_up, e_down, chunks):
    _, n_experts, width, dim = e_gate.shape
    rows = n_all.shape[0] // chunks - TILE
    seq = rows * chunks
    n_rows = TILE * BLOCK_TILES
    shared = pl.BlockSpec((1, width, dim), lambda e, *_: (layer, 0, 0))
    routed = pl.BlockSpec((1, 1, width, dim), lambda e, *_: (layer, e, 0, 0))
    anywhere = pl.BlockSpec(memory_space=pl.ANY)
    grid_spec = pltpu.PrefetchScalarGridSpec(
        num_scalar_prefetch=5,
        grid=(n_experts,),
        in_specs=[anywhere, anywhere, shared, shared, shared, routed, routed, routed],
        out_specs=anywhere,
        scratch_shapes=[
            pltpu.VMEM((seq, dim), jnp.bfloat16),
            pltpu.VMEM((seq, 2 * width), jnp.float32),
            pltpu.VMEM((seq + TILE, dim), jnp.bfloat16),
            pltpu.VMEM((4 * width, dim), jnp.bfloat16),
            pltpu.VMEM((4 * width, dim), jnp.bfloat16),
            pltpu.VMEM((n_rows, dim), jnp.bfloat16),
            pltpu.VMEM((n_rows, 2 * width), jnp.float32),
            pltpu.SemaphoreType.DMA((chunks + 1,)),
            pltpu.SemaphoreType.DMA,
        ],
    )
    return pl.pallas_call(
        expert_kernel,
        grid_spec=grid_spec,
        out_shape=jax.ShapeDtypeStruct((seq, dim), jnp.bfloat16),
        compiler_params=pltpu.CompilerParams(vmem_limit_bytes=50 * 1024 * 1024),
        cost_estimate=pl.CostEstimate(flops=2 * 13500 * dim * 512, bytes_accessed=4 * seq * dim + 6 * n_experts * width * dim, transcendentals=0),
        name="experts",
    )(*lists, n_all, p_all, s_gate, s_up, s_down, e_gate, e_up, e_down)


def sort_rows(n_act, gate_val, route, n_experts):
    rows, dim = n_act.shape
    onehot = (route[:, None] == jnp.arange(n_experts)[None, :]).astype(jnp.bfloat16)
    earlier = (jnp.arange(rows)[:, None] > jnp.arange(rows)[None, :]).astype(jnp.bfloat16)
    rank = jnp.dot(earlier, onehot, preferred_element_type=jnp.float32)
    smaller = jnp.sum((route[None, :] < jnp.arange(n_experts)[:, None]).astype(jnp.float32), axis=1)
    pos = jnp.sum(onehot.astype(jnp.float32) * (rank + smaller[None, :]), axis=1).astype(jnp.int32)
    perm = pos[None, :] == jnp.arange(rows)[:, None]
    n_sorted = jnp.dot(perm.astype(jnp.bfloat16), n_act, preferred_element_type=jnp.float32).astype(jnp.bfloat16)
    gate_sorted = jnp.sum(jnp.where(perm, gate_val[None, :], 0.0), axis=1)
    high = gate_sorted.astype(jnp.bfloat16)
    low = (gate_sorted - high.astype(jnp.float32)).astype(jnp.bfloat16)
    extra = jnp.pad(jnp.concatenate([high, low])[None, :], ((0, TILE - 1), (0, dim - 2 * rows)))
    return jnp.concatenate([n_sorted, extra], axis=0), perm


def solution(mesh):
    seq_spec = P(("dp", "tp"), None)
    in_specs = (seq_spec, P(None, ("dp", "tp")), P(None, None, "tp"), P(None, "tp"), P(None, "tp"), P(None, "tp", None), P(None, None), P(None), P(None, None, None), P(None, None, "tp"), P(None, None, "tp"), P(None, "tp", None), P(None, None, None, "tp"), P(None, None, None, "tp"), P(None, None, "tp", None))
    out_specs = (seq_spec, P("dp", "tp", None), P("dp", "tp", None))
    chunks = mesh.shape["tp"]

    def per_device(hidden, routes, w_query, w_key, w_value, w_out, q_gain, k_gain, w_router, shared_gate, shared_up, shared_down, expert_gate, expert_up, expert_down):
        head_dim = q_gain.shape[1]
        n_experts = w_router.shape[2]
        rows, dim = hidden.shape
        seq_len = rows * chunks
        n_layers = w_query.shape[0]
        wq_t = jnp.swapaxes(w_query, 1, 2)
        s_gate, s_up = jnp.swapaxes(shared_gate, 1, 2), jnp.swapaxes(shared_up, 1, 2)
        e_gate, e_up = jnp.swapaxes(expert_gate, 2, 3), jnp.swapaxes(expert_up, 2, 3)

        routes_all = lax.all_gather(routes, "tp", axis=1, tiled=True)
        lists = tile_lists(routes_all, chunks, n_experts)
        cos_t, sin_t = rope_tables_t(seq_len, head_dim)

        a_all = lax.all_gather(rms_norm(hidden).astype(jnp.bfloat16), "tp", axis=0, tiled=True)
        q_raw, k_t, v_t = qkv_proj(a_all, wq_t, w_key.T, w_value.T, cos_t, sin_t, k_gain, chunks)
        small_v = jnp.max(jnp.abs(v_t)).astype(jnp.float32) <= VALUE_BOUND

        wq_t, w_out, q_raw = lax.optimization_barrier((wq_t, w_out, q_raw))
        wo_full = [lax.all_gather(w_out[layer], "tp", axis=0, tiled=True) for layer in range(n_layers)]
        wq_full = {layer: lax.all_gather(wq_t[layer], "tp", axis=0, tiled=True) for layer in range(1, n_layers)}

        state = hidden
        for layer in range(n_layers):
            if layer:
                a_act = rms_norm(state).astype(jnp.bfloat16)
                q_full = lax.dot_general(wq_full[layer], a_act, NT, preferred_element_type=jnp.float32).astype(jnp.bfloat16)
                q_raw = lax.all_to_all(q_full.reshape(chunks, -1, rows), "tp", 0, 0, tiled=True)
            bound = 1.02 * head_dim**0.5 * jnp.max(jnp.abs(q_gain[layer])) * jnp.max(jnp.abs(k_gain))
            fast = ((bound <= SCORE_BOUND) & small_v).astype(jnp.int32)[None]
            o_t = attention(fast, q_raw, k_t, v_t, cos_t, sin_t, q_gain[layer])
            o_t = lax.all_to_all(o_t, "tp", 0, 0, tiled=True).reshape(-1, rows)
            attn = lax.dot_general(o_t, wo_full[layer], TN, preferred_element_type=jnp.float32)
            state = (state.astype(jnp.float32) + attn).astype(jnp.bfloat16)

            n_act = rms_norm(state).astype(jnp.bfloat16)
            router_probs = jax.nn.softmax(jnp.dot(n_act, w_router[layer], preferred_element_type=jnp.float32), axis=-1)
            gate_val = jnp.sum(jnp.where(routes[layer][:, None] == jnp.arange(n_experts)[None, :], router_probs, 0.0), axis=1)
            payload, perm = sort_rows(n_act, gate_val, routes[layer], n_experts)
            n_all = lax.all_gather(payload, "tp", axis=0, tiled=True)
            gates = n_all.reshape(chunks, rows + TILE, dim)[:, rows, : 2 * rows].astype(jnp.float32)
            gates = (gates[:, :rows] + gates[:, rows:]).reshape(seq_len, 1)
            p_all = jnp.broadcast_to(gates, (seq_len, 2 * s_gate.shape[1]))
            part = experts([vals[layer] for vals in lists], layer, n_all, p_all, s_gate, s_up, shared_down, e_gate, e_up, expert_down, chunks)
            moe = lax.psum_scatter(part, "tp", scatter_dimension=0, tiled=True)
            moe = lax.dot_general(perm.astype(jnp.bfloat16), moe, TN, preferred_element_type=jnp.float32)
            state = (state.astype(jnp.float32) + moe).astype(jnp.bfloat16)
        return (state, k_t.T[:, None, :], v_t.T[:, None, :])

    return jax.shard_map(per_device, mesh=mesh, in_specs=in_specs, out_specs=out_specs, check_vma=False)
```

time: 2000 us -> 812 us (0.41)
  matrix products: 553 us -> 28.1 us
  other arithmetic: 434 us -> 16.2 us
  local copies, waits for them, and re-layouts: 289 us -> 9.21 us
  Pallas kernels: 269 us -> 295 us
    dot_general x76 -> x11, matrix products: 553 us -> 28.1 us  [the longest x2 10.9 us: per_device(): lax.dot_general(o_t, wo_full[layer], TN, preferred_element_type=jnp.float32)]
    pallas_call x0 -> x5, Pallas kernels: none -> 295 us  [the longest x2 148 us: experts(): pl.pallas_call(expert_kernel, grid_spec=grid_spec, out_shape=jax.ShapeDty...]
    reduce_sum x36 -> x10, other arithmetic: 266 us -> 2.34 us  [the longest x1 1.22 us: pick(): return jnp.sum(jnp.where(hit, vals, 0), axis=-1)]
    another operation x6 -> x0, Pallas kernels: 263 us -> none
    reduce_scatter x4 -> x2, waiting for transfers between devices: 275 us -> 136 us  [per_device(): moe = lax.psum_scatter(part, 'tp', scatter_dimension=0, tiled=True)]
    gather x4 -> x0, local copies, waits for them, and re-layouts: 134 us -> none  [the longest x2 71.4 us: routed_experts(): return jnp.take(sorted_out, inverse, axis=0) * gate_val[:, None]]
    all_gather x4 -> x6, waiting for transfers between devices: 131 us -> 209 us  [the longest x2 114 us: per_device(): n_all = lax.all_gather(payload, 'tp', axis=0, tiled=True)]
    all_to_all x0 -> x3, waiting for transfers between devices: none -> 75.3 us  [the longest x2 39.9 us: per_device(): o_t = lax.all_to_all(o_t, 'tp', 0, 0, tiled=True).reshape(-1, rows)]
  transfers between devices with their start and end apart: 8 -> 11, of which waited for: 6 -> 9; matrix products, arithmetic and copies ran while one was open for 10% -> 3% of each run, Pallas kernels for 0% -> 17%
where the time goes in v1:
time: 812 us; the launch traced here: 814 us
  waiting for transfers between devices  422 us (52%)
  Pallas kernels  295 us (36%)
  matrix products  28.1 us (3%)
  between operations  17.5 us (2%)
  other arithmetic  16.2 us (2%)
  blocking collectives  14 us (2%)
  starting transfers between devices  12.6 us (2%)
  local copies, waits for them, and re-layouts  9.21 us (1%)
    pallas_call x2, Pallas kernels, experts(): pl.pallas_call(expert_kernel, grid_spec=grid_spec, out_shape=jax.ShapeDty...  148 us
    reduce_scatter x2, waiting for transfers between devices, per_device(): moe = lax.psum_scatter(part, 'tp', scatter_dimension=0, tiled=True)  136 us
    pallas_call x2, Pallas kernels, attention(): pl.pallas_call(attention_kernel, grid_spec=grid_spec, out_shape=jax.Shape...  136 us
    all_gather x2, waiting for transfers between devices, per_device(): n_all = lax.all_gather(payload, 'tp', axis=0, tiled=True)  114 us
    all_gather x1, waiting for transfers between devices, per_device(): lax.all_gather(rms_norm(hidden).astype(jnp.bfloat16), 'tp', axis=0, tiled...  65.3 us
    all_to_all x2, waiting for transfers between devices, per_device(): o_t = lax.all_to_all(o_t, 'tp', 0, 0, tiled=True).reshape(-1, rows)  39.9 us
    all_to_all x1, waiting for transfers between devices, per_device(): lax.all_to_all(q_full.reshape(chunks, -1, rows), 'tp', 0, 0, tiled=True)  35.4 us
    all_gather x1, waiting for transfers between devices, per_device(): lax.all_gather(wq_t[layer], 'tp', axis=0, tiled=True)  29.7 us
  transfers between devices with their start and end apart: 11, of which 9 were waited for; matrix products, arithmetic and copies ran while one was open for 3% of the time, Pallas kernels for 17%

profile of v1, /device:TPU:81, one launch (start us, length us, event | category | flops | bytes accessed | tf_op | source)
XLA Modules:
  0.0 814.0 jit_solution(12162140480310666167)
XLA Ops:
  7.3 1.9 fusion.8
  9.2 1.5 fusion.9
  10.8 0.7 copy.37.kg_ref
  11.5 2.8 fusion.46
  14.3 65.3 %all-gather.10.cloned.1.call-done.a_ref = bf16[4096,1536]{1,0:T(8,128)(2,1)} async-done(((bf16[512,1536]{1,0:T(8,128)(2,1)}), bf16[4096,1536]{1,0:T(8,128)(2,1)}) %all-gather.10.cloned.1.call-update) | async-done | bytes 12582928 | tf_op jit(solution)/shard_map/all_gather | solution.py:397
  79.7 11.1 %qkv.1 = (bf16[8,192,512]{2,1,0:T(8,128)(2,1)}, bf16[64,4096]{1,0:T(8,128)(2,1)}, bf16[64,4096]{1,0:T(8,128)(2,1)}) custom-call(bf16[4096,1536]{1,0:T(8,128)(2,1)} %all-gather.10.cloned.1.call-done.a_ref, bf16[2,192,1536]{2,1,0:T(8,128)(2,1)} %bitcast.108, bf16[64,1536]{1,0:T(8,128)(2,1)} %bitcast.114, bf16[64,1536]{1,0:T(8,128)(2,1)} %bitcast.115, ...), custom_call_target="tpu_custom_call" | custom-call | flops 4026531840 | bytes 12582912 | tf_op jit(solution)/shard_map/qkv/pallas_call | solution.py:64
  90.8 1.1 fusion.67
  92.0 0.6 abs_reduce_fusion.1
  92.6 0.7 copy.38.qg_ref
  93.9 0.6 abs_reduce_fusion.2
  95.0 0.6 abs_reduce_fusion
  96.2 67.8 %attention.2 = bf16[8,192,512]{2,1,0:T(8,128)(2,1)} custom-call(s32[1]{0:T(128)} %bitcast.4.fast_ref, bf16[8,192,512]{2,1,0:T(8,128)(2,1)} %get-tuple-element.11.q_ref, bf16[64,4096]{1,0:T(8,128)(2,1)} %get-tuple-element.12.k_ref, bf16[64,4096]{1,0:T(8,128)(2,1)} %get-tuple-element.9.v_ref, f32[32,4096]{1,0:T(8,128)} %get-tuple-element.51.cos_ref, ...), custom_call_target="tpu_custom_call" | custom-call | flops 25769803776 | bytes 6291456 | tf_op jit(solution)/shard_map/attention/pallas_call | solution.py:203
  164.0 3.9 all-to-all-start
  168.5 19.9 %all-to-all-done = bf16[8,192,512]{2,1,0:T(8,128)(2,1)S(1)} async-done(((bf16[8,192,512]{2,1,0:T(8,128)(2,1)}), bf16[8,192,512]{2,1,0:T(8,128)(2,1)S(1)}, u32[]{:S(2)}, u32[]{:S(2)}) %all-to-all-start) | async-done | bytes 1572896 | tf_op jit(solution)/shard_map/all_to_all | solution.py:414
  188.4 5.3 fusion.11
  193.7 0.7 fusion.69
  194.5 1.1 convolution_convert_fusion.1
  195.8 1.3 fusion.28
  197.2 14.0 %all_gather.23 = s32[2,4096]{1,0:T(2,128)S(1)} all-gather(s32[2,512]{1,0:T(2,128)S(1)} %copy-done.8), channel_id=1, replica_groups=mesh['dp'=4,'tp'=8] {'tp'}, dimensions={1}, use_global_device_ids=true | all-gather | bytes 36864 | tf_op jit(solution)/shard_map/all_gather | solution.py:393
  212.3 0.6 reduce-window.6
  214.3 1.2 select_reduce_fusion
  215.8 47.7 %all-gather.12.cloned.1.call-done.n_hbm = bf16[4224,1536]{1,0:T(8,128)(2,1)} async-done(((bf16[528,1536]{1,0:T(8,128)(2,1)}), bf16[4224,1536]{1,0:T(8,128)(2,1)}) %all-gather.12.cloned.1.call-update) | async-done | bytes 12976144 | tf_op jit(solution)/shard_map/all_gather | solution.py:422
  263.6 0.9 slice_convert_fusion.1
  264.5 0.6 broadcast_in_dim.156.p_hbm
  265.2 74.6 %experts.2 = bf16[4096,1536]{1,0:T(8,128)(2,1)} custom-call(s32[592]{0:T(1024)S(1)} %get-tuple-element.28.tiles_ref, s32[592]{0:T(1024)S(1)} %get-tuple-element.63.low_ref, s32[592]{0:T(1024)S(1)} %get-tuple-element.24.high_ref, s32[40]{0:T(128)S(1)} %get-tuple-element.65.start_ref, s32[40]{0:T(128)S(1)} %get-tuple-element.15.stop_ref, ...), custom_call_target="tpu_custom_call" | custom-call | flops 21233664000 | bytes 48758784 | tf_op jit(solution)/shard_map/experts/pallas_call | solution.py:351
  339.9 1.1 copy-done.4
  341.1 0.9 slice.111
  342.6 67.3 %reduce-scatter.3.cloned.1.call-done = bf16[512,1536]{1,0:T(8,128)(2,1)} async-done(((bf16[4096,1536]{1,0:T(8,128)(2,1)}), bf16[512,1536]{1,0:T(8,128)(2,1)}) %reduce-scatter.3.cloned.1.call-update) | async-done | bytes 1572880 | tf_op jit(solution)/shard_map/reduce_scatter | solution.py:427
  409.9 3.1 fusion.13
  413.1 29.7 %all-gather.18.cloned.1.call-done = bf16[1,1536,1536]{2,1,0:T(8,128)(2,1)} async-done(((bf16[1,192,1536]{2,1,0:T(8,128)(2,1)}), bf16[1,1536,1536]{2,1,0:T(8,128)(2,1)}) %all-gather.18.cloned.1.call-update) | async-done | bytes 4718608 | tf_op jit(solution)/shard_map/all_gather | solution.py:403
  442.8 6.3 fusion.22
  449.1 3.9 all-to-all-start.1
  454.1 0.7 copy.44.qg_ref
  454.8 35.4 %all-to-all-done.1.q_ref = bf16[8,192,512]{2,1,0:T(8,128)(2,1)S(1)} async-done(((bf16[8,192,512]{2,1,0:T(8,128)(2,1)}), bf16[8,192,512]{2,1,0:T(8,128)(2,1)S(1)}, u32[]{:S(2)}, u32[]{:S(2)}) %all-to-all-start.1) | async-done | bytes 1572896 | tf_op jit(solution)/shard_map/all_to_all | solution.py:410
  490.2 1.1 copy-done.5
  491.4 67.8 %attention.3 = bf16[8,192,512]{2,1,0:T(8,128)(2,1)} custom-call(s32[1]{0:T(128)} %bitcast.21.fast_ref, bf16[8,192,512]{2,1,0:T(8,128)(2,1)} %copy-done.5, bf16[64,4096]{1,0:T(8,128)(2,1)} %get-tuple-element.12.k_ref, bf16[64,4096]{1,0:T(8,128)(2,1)} %get-tuple-element.9.v_ref, f32[32,4096]{1,0:T(8,128)} %get-tuple-element.51.cos_ref, ...), custom_call_target="tpu_custom_call" | custom-call | flops 25769803776 | bytes 6291456 | tf_op jit(solution)/shard_map/attention/pallas_call | solution.py:203
  559.1 4.3 all-to-all-start.2
  563.8 20.0 %all-to-all-done.2 = bf16[8,192,512]{2,1,0:T(8,128)(2,1)S(1)} async-done(((bf16[8,192,512]{2,1,0:T(8,128)(2,1)}), bf16[8,192,512]{2,1,0:T(8,128)(2,1)S(1)}, u32[]{:S(2)}, u32[]{:S(2)}) %all-to-all-start.2) | async-done | bytes 1572896 | tf_op jit(solution)/shard_map/all_to_all | solution.py:414
  583.9 5.6 fusion.16
  589.6 0.7 fusion.70
  590.2 1.1 convolution_convert_fusion
  591.7 1.3 fusion.29
  593.1 66.3 %all-gather.14.cloned.1.call-done.n_hbm = bf16[4224,1536]{1,0:T(8,128)(2,1)} async-done(((bf16[528,1536]{1,0:T(8,128)(2,1)}), bf16[4224,1536]{1,0:T(8,128)(2,1)}) %all-gather.14.cloned.1.call-update) | async-done | bytes 12976144 | tf_op jit(solution)/shard_map/all_gather | solution.py:422
  659.4 0.9 slice_convert_fusion
  660.3 0.6 broadcast_in_dim.162.p_hbm
  660.9 73.5 %experts.3 = bf16[4096,1536]{1,0:T(8,128)(2,1)} custom-call(s32[592]{0:T(1024)S(1)} %get-tuple-element.29.tiles_ref, s32[592]{0:T(1024)S(1)} %get-tuple-element.62.low_ref, s32[592]{0:T(1024)S(1)} %get-tuple-element.25.high_ref, s32[40]{0:T(128)S(1)} %get-tuple-element.64.start_ref, s32[40]{0:T(128)S(1)} %get-tuple-element.16.stop_ref, ...), custom_call_target="tpu_custom_call" | custom-call | flops 21233664000 | bytes 48758784 | tf_op jit(solution)/shard_map/experts/pallas_call | solution.py:351
  734.6 69.1 %reduce-scatter.5.cloned.1.call-done = bf16[512,1536]{1,0:T(8,128)(2,1)} async-done(((bf16[4096,1536]{1,0:T(8,128)(2,1)}), bf16[512,1536]{1,0:T(8,128)(2,1)}) %reduce-scatter.5.cloned.1.call-update) | async-done | bytes 1572880 | tf_op jit(solution)/shard_map/reduce_scatter | solution.py:427
  803.6 3.6 fusion.26
  (107 shorter events, 5.6 us)
Async XLA Ops:
  7.2 2.0 copy-start.3
  7.2 72.5 %all-gather.10.cloned.1.call-start = ((), (), s32[]{:S(2)}) async-start(), calls=%async_computation.5 | async-start | bytes 14155776 | tf_op jit(solution)/shard_map/all_gather | solution.py:397
  9.2 1.6 copy-start.10
  10.7 177.7 %all-gather.16.cloned.1.call-start = ((), (), s32[]{:S(2)}) async-start(), calls=%async_computation.10 | async-start | bytes 5308416 | tf_op jit(solution)/shard_map/all_gather | solution.py:402
  79.7 11.1 %copy-start.6 = (bf16[2,192,1536]{2,1,0:T(8,128)(2,1)S(1)}, bf16[2,192,1536]{2,1,0:T(8,128)(2,1)}, u32[]{:S(2)}) copy-start(bf16[2,192,1536]{2,1,0:T(8,128)(2,1)} %param.20) | copy-start | bytes 3538948
  90.8 1.2 copy-start.9
  90.8 4.2 copy-start.7
  164.0 4.1 copy-start.8
  164.0 24.4 %all-to-all-start = ((bf16[8,192,512]{2,1,0:T(8,128)(2,1)}), bf16[8,192,512]{2,1,0:T(8,128)(2,1)S(1)}, u32[]{:S(2)}, u32[]{:S(2)}) async-start(bf16[8,192,512]{2,1,0:T(8,128)(2,1)} %attention.2), calls=%async_computation | async-start | bytes 3145728 | tf_op jit(solution)/shard_map/all_to_all | solution.py:414
  167.9 95.7 %all-gather.12.cloned.1.call-start = ((), (), s32[]{:S(2)}) async-start(), calls=%async_computation.6 | async-start | bytes 14598144 | tf_op jit(solution)/shard_map/all_gather | solution.py:422
  188.4 5.3 copy-start.11
  193.7 1.9 copy-start.12
  197.2 212.8 %reduce-scatter.3.cloned.1.call-start = ((), (), s32[]{:S(2)}) async-start(), calls=%async_computation.7 | async-start | bytes 14155776 | tf_op jit(solution)/shard_map/reduce_scatter | solution.py:427
  211.2 53.9 %copy-start = (bf16[2,1536,64]{1,2,0:T(8,128)(2,1)S(1)}, bf16[2,1536,64]{1,2,0:T(8,128)(2,1)}, u32[]{:S(2)}) copy-start(bf16[2,1536,64]{1,2,0:T(8,128)(2,1)} %param.24) | copy-start | bytes 1179652
  211.3 53.9 %copy-start.1 = (bf16[2,1536,64]{1,2,0:T(8,128)(2,1)S(1)}, bf16[2,1536,64]{1,2,0:T(8,128)(2,1)}, u32[]{:S(2)}) copy-start(bf16[2,1536,64]{1,2,0:T(8,128)(2,1)} %param.25) | copy-start | bytes 1179652
  211.3 53.9 %copy-start.2 = (bf16[2,64,1536]{2,1,0:T(8,128)(2,1)S(1)}, bf16[2,64,1536]{2,1,0:T(8,128)(2,1)}, u32[]{:S(2)}) copy-start(bf16[2,64,1536]{2,1,0:T(8,128)(2,1)} %sd_ref.3) | copy-start | bytes 1179652
  339.8 1.3 copy-start.4
  339.9 102.9 %all-gather.18.cloned.1.call-start = ((), (), s32[]{:S(2)}) async-start(), calls=%async_computation.11 | async-start | bytes 5308416 | tf_op jit(solution)/shard_map/all_gather | solution.py:403
  342.0 221.9 %all-gather.20.cloned.1.call-start = ((), (), s32[]{:S(2)}) async-start(), calls=%async_computation.12 | async-start | bytes 5308416 | tf_op jit(solution)/shard_map/all_gather | solution.py:402
  413.0 36.0 %copy-start.15 = (bf16[512,1536]{1,0:T(8,128)(2,1)}, bf16[512,1536]{1,0:T(8,128)(2,1)S(1)}, u32[]{:S(2)}) copy-start(bf16[512,1536]{1,0:T(8,128)(2,1)S(1)} %get-tuple-element.57) | copy-start | bytes 4718596
  449.1 41.1 %all-to-all-start.1 = ((bf16[8,192,512]{2,1,0:T(8,128)(2,1)}), bf16[8,192,512]{2,1,0:T(8,128)(2,1)S(1)}, u32[]{:S(2)}, u32[]{:S(2)}) async-start(bf16[8,192,512]{2,1,0:T(8,128)(2,1)} %bitcast.112), calls=%async_computation.2 | async-start | bytes 3145728 | tf_op jit(solution)/shard_map/all_to_all | solution.py:410
  490.2 1.1 copy-start.5
  559.1 24.7 %all-to-all-start.2 = ((bf16[8,192,512]{2,1,0:T(8,128)(2,1)}), bf16[8,192,512]{2,1,0:T(8,128)(2,1)S(1)}, u32[]{:S(2)}, u32[]{:S(2)}) async-start(bf16[8,192,512]{2,1,0:T(8,128)(2,1)} %attention.3), calls=%async_computation.3 | async-start | bytes 3145728 | tf_op jit(solution)/shard_map/all_to_all | solution.py:414
  563.4 96.0 %all-gather.14.cloned.1.call-start = ((), (), s32[]{:S(2)}) async-start(), calls=%async_computation.8 | async-start | bytes 14598144 | tf_op jit(solution)/shard_map/all_gather | solution.py:422
  589.5 1.8 copy-start.13
  593.0 210.6 %reduce-scatter.5.cloned.1.call-start = ((), (), s32[]{:S(2)}) async-start(), calls=%async_computation.9 | async-start | bytes 14155776 | tf_op jit(solution)/shard_map/reduce_scatter | solution.py:427
  734.5 69.1 %copy-start.14 = (bf16[512,1536]{1,0:T(8,128)(2,1)S(1)}, bf16[512,1536]{1,0:T(8,128)(2,1)}, u32[]{:S(2)}) copy-start(bf16[512,1536]{1,0:T(8,128)(2,1)} %copy-done.13) | copy-start | bytes 4718596
Sparse Core Ops, SparseCore 0:
  10.8 68.8 all-gather.9
  92.1 31.1 all-gather.15
  197.3 66.2 all-gather.11
  340.0 69.9 reduce-scatter.2
  411.4 31.3 all-gather.17
  444.2 47.5 all-gather.19
  593.1 66.1 all-gather.13
  734.7 68.8 reduce-scatter.4
